TPU v7x, 128 devices: a whole 4x4x4 slice. The times are simulated.
128 devices in a mesh: dp: 16 (over y, z), vocab: 8 (over x, core).
Axes of the slice: x: 4, y: 4, z: 4, core: 2. Of those that a mesh axis runs over, the one named last changes fastest.
Arguments:
- tokens: bfloat16 [2048, 7168], P('dp'), may hold values from -6 to 6
- expert_hidden: bfloat16 [2048, 8, 1024], P('dp'), may hold values from -6 to 6
- routes: int32 [2048, 8], P('dp'), may hold values from 0 to 63, all different within a row; in each aligned block of 16 rows (0 to 15, 16 to 31, ...) at most 3 rows name the same one
- route_weight: float32 [2048, 8], P('dp'), may hold values from 0.05 to 0.45
- expert_weight: bfloat16 [128, 512, 7168], P(('dp', 'vocab')), may hold values from -0.1875 to 0.1875
- norm_gain: float32 [7168], replicated, may hold values from 0.5 to 1.5
- head_weight: bfloat16 [7168, 114688], P(None, ('dp', 'vocab')), may hold values from -8 to 8
- targets: int32 [2048], P('dp'), may hold values from 0 to 114687
- rollout_logprob: float32 [2048], P('dp'), may hold values from -21 to -13
- advantages: float32 [2048], P('dp'), may hold values from -5 to 5
Outputs:
- layer_out: bfloat16 [2048, 7168], P('dp')
- token_logprob: float32 [2048], P('dp')
- token_loss: float32 [2048], P('dp')
Inputs may be any that keep to these rules, and one draw needn't show every extreme that they name: The 8 routes of a token name different experts; among the routes of one aligned block of 16 token rows, no expert is named more than 3 times.
All inputs are finite; a program needn't handle non-finite values.
Results may differ from a plain program's by a relative error of at most 0.02.
Values may be sent and summed in bfloat16 or wider, within the bound.
No kernel may reach another device: no remote copies, remote signals or barrier semaphores. Data moves between devices by JAX's collectives and lax.ppermute only.
A program may use at most 192 MiB of HBM per device.

v0:
```python
import jax
import jax.numpy as jnp
from jax import lax
from jax.sharding import Mesh
from jax.sharding import PartitionSpec as P

VOCAB = ("vocab_0", "vocab_1")
DP_VOCAB = ("dp_0", "dp_1", "vocab_0", "vocab_1")
DP = ("dp_0", "dp_1")


norm_epsilon = 1e-06
clip_low = 0.8
clip_high = 1.2
dual_bound = 3.0


def sent_to_all(shard, axis):
    peers = lax.axis_size(axis)
    return lax.all_to_all(
        jnp.broadcast_to(shard[None], (peers, *shard.shape)), axis, 0, 0, tiled=True
    )


def joined_along(tiles, dim):
    dims = list(tiles.shape[1:])
    dims[dim] *= tiles.shape[0]
    return jnp.moveaxis(tiles, 0, dim).reshape(dims)


def collect(shard, axis, dim):
    tiles = sent_to_all(shard, axis)
    return joined_along(tiles, dim)


def all_in_one(shard, axis):
    leaves = jax.tree.leaves(shard)
    sequence = sorted(range(len(leaves)), key=lambda k: -leaves[k].size)
    width = (1, *leaves[sequence[0]].shape)[-1]
    lines = [
        jnp.pad(leaves[k].reshape(-1), (0, -leaves[k].size % width)).reshape(-1, width)
        for k in sequence
    ]
    both, at, found = (lax.all_gather(jnp.concatenate(lines), axis), 0, {})
    for k, line in zip(sequence, lines):
        share = both[:, at : at + len(line)].reshape(len(both), -1)
        found[k] = share[:, : leaves[k].size].reshape(-1, *leaves[k].shape)
        at += len(line)
    numbers = iter(range(len(leaves)))
    return jax.tree.map(lambda _: found[next(numbers)], shard)


def combined_by_axis(shard, axes, combine):
    for axis in axes:
        pieces = all_in_one(shard, axis)
        shard = jax.tree.map(lambda part: part[0], pieces)
        for k in range(1, lax.axis_size(axis)):
            shard = combine(shard, jax.tree.map(lambda part: part[k], pieces))
    return shard


def rms_scale(values, norm_gain):
    widened = values.astype(jnp.float32)
    mean_square = jnp.mean(widened * widened, axis=-1, keepdims=True)
    return (widened * lax.rsqrt(mean_square + norm_epsilon) * norm_gain).astype(jnp.bfloat16)


def clipped_loss(logprob, rollout_logprob, advantages):
    ratio = jnp.exp(logprob - rollout_logprob)
    surrogate = jnp.minimum(ratio * advantages, jnp.clip(ratio, clip_low, clip_high) * advantages)
    bounded = jnp.where(
        advantages < 0.0, jnp.maximum(surrogate, dual_bound * advantages), surrogate
    )
    return -bounded


def combine_stats(earlier, later):
    peak_one, total_one, picked_one = earlier
    peak_two, total_two, picked_two = later
    highest = jnp.maximum(peak_one, peak_two)
    merged_total = total_one * jnp.exp(peak_one - highest) + total_two * jnp.exp(peak_two - highest)
    return (highest, merged_total, picked_one + picked_two)


def per_device(
    tokens,
    expert_hidden,
    routes,
    route_weight,
    expert_weight,
    norm_gain,
    head_weight,
    targets,
    rollout_logprob,
    advantages,
):
    vocab_count = lax.axis_size(VOCAB)
    device_count = lax.axis_size(DP_VOCAB)
    experts = device_count // 2
    group_count = tokens.shape[0]
    sub_rows = group_count // vocab_count
    top_count = routes.shape[1]
    capacity = max(2, 3 * sub_rows * top_count // (2 * experts))
    sub_start = lax.axis_index(VOCAB) * sub_rows
    mine_tokens = lax.dynamic_slice_in_dim(tokens, sub_start, sub_rows, 0)
    mine_hidden = lax.dynamic_slice_in_dim(expert_hidden, sub_start, sub_rows, 0)
    mine_routes = lax.dynamic_slice_in_dim(routes, sub_start, sub_rows, 0)
    mine_weights = lax.dynamic_slice_in_dim(route_weight, sub_start, sub_rows, 0)
    route_list = mine_routes.reshape(-1)
    onehot = (route_list[:, None] == lax.iota(jnp.int32, experts)[None, :]).astype(jnp.int32)
    before = jnp.cumsum(onehot, axis=0) - onehot
    slot_index = jnp.sum(before * onehot, axis=1)
    position = route_list * capacity + slot_index
    select = (lax.iota(jnp.int32, experts * capacity)[:, None] == position[None, :]).astype(
        jnp.bfloat16
    )
    hidden_rows = mine_hidden.reshape(-1, mine_hidden.shape[2])
    half_width = hidden_rows.shape[1] // 2
    lower_buffer = jnp.dot(
        select, hidden_rows[:, :half_width], preferred_element_type=jnp.float32
    ).astype(jnp.bfloat16)
    upper_buffer = jnp.dot(
        select, hidden_rows[:, half_width:], preferred_element_type=jnp.float32
    ).astype(jnp.bfloat16)
    lower_buffer = lower_buffer.reshape(experts, capacity, half_width)
    upper_buffer = upper_buffer.reshape(experts, capacity, half_width)
    buffer = jnp.stack((lower_buffer, upper_buffer), axis=1).reshape(
        device_count, capacity, half_width
    )
    weight_local = expert_weight[0]
    received = lax.all_to_all(buffer, DP_VOCAB, split_axis=0, concat_axis=0, tiled=True)
    sources, slot_count, width = received.shape
    product = jnp.dot(
        received.reshape(sources * slot_count, width),
        weight_local,
        preferred_element_type=jnp.float32,
    ).astype(jnp.bfloat16)
    returned = lax.all_to_all(
        product.reshape(sources, slot_count, -1), DP_VOCAB, split_axis=0, concat_axis=0, tiled=True
    )
    model_width = returned.shape[2]
    returned = returned.reshape(experts, 2, capacity, model_width)
    lower_back = returned[:, 0].reshape(experts * capacity, model_width)
    upper_back = returned[:, 1].reshape(experts * capacity, model_width)
    contract = (((0,), (0,)), ((), ()))
    route_out = lax.dot_general(select, lower_back, contract, preferred_element_type=jnp.float32)
    route_out = route_out + lax.dot_general(
        select, upper_back, contract, preferred_element_type=jnp.float32
    )
    moe = jnp.sum(
        route_out.reshape(sub_rows, top_count, model_width) * mine_weights[:, :, None], axis=1
    )
    layer_sub = (mine_tokens.astype(jnp.float32) + moe).astype(jnp.bfloat16)
    group_layer = collect(layer_sub, VOCAB, 0)
    voc_dev = head_weight.shape[1]
    column_start = lax.axis_index(DP_VOCAB) * voc_dev
    normed_sub = rms_scale(layer_sub, norm_gain)
    labels_sub = lax.dynamic_slice_in_dim(targets, sub_start, sub_rows, 0)
    normed = lax.all_gather(normed_sub, DP_VOCAB, axis=0, tiled=True)
    labels = lax.all_gather(labels_sub, DP_VOCAB, axis=0, tiled=True)
    logits = jnp.dot(normed, head_weight, preferred_element_type=jnp.float32)
    row_peak = jnp.max(logits, axis=1)
    row_total = jnp.sum(jnp.exp(logits - row_peak[:, None]), axis=1)
    columns = column_start + lax.iota(jnp.int32, voc_dev)
    picked = jnp.sum(jnp.where(columns[None, :] == labels[:, None], logits, 0.0), axis=1)
    peak_all = row_peak
    total_all = row_total
    picked_all = picked
    row_stats = (peak_all, total_all, picked_all)
    peak_all, total_all, picked_all = row_stats
    global_peak, sum_total, target_logit = combined_by_axis(
        (peak_all, total_all, picked_all), DP_VOCAB, combine_stats
    )
    log_total = global_peak + jnp.log(sum_total)
    logprob_all = target_logit - log_total
    group_start = lax.axis_index(DP) * group_count
    token_logprob = lax.dynamic_slice_in_dim(logprob_all, group_start, group_count, 0)
    token_loss = clipped_loss(token_logprob, rollout_logprob, advantages)
    return (group_layer, token_logprob, token_loss)


def solution(mesh):
    torus = Mesh(mesh.devices.reshape(4, 4, 4, 2), ("dp_0", "dp_1", "vocab_0", "vocab_1"))
    placed = (
        P(DP, None),
        P(DP, None, None),
        P(DP, None),
        P(DP, None),
        P(DP_VOCAB, None, None),
        P(),
        P(None, DP_VOCAB),
        P(DP),
        P(DP),
        P(DP),
    )
    return jax.shard_map(
        per_device,
        mesh=torus,
        in_specs=placed,
        out_specs=(P(DP, None), P(DP), P(DP)),
        check_vma=False,
    )
```

profile of v0, /device:TPU:1, one launch (start us, length us, event | category | flops | bytes accessed | tf_op | source)
XLA Modules:
  0.0 378.0 jit_solution(2879666834598453781)
XLA Ops:
  7.2 0.9 constant_dynamic-slice_fusion.1
  10.0 24.9 %all_to_all.15 = bf16[128,3,512]{2,1,0:T(4,128)(2,1)S(1)} all-to-all(bf16[128,3,512]{2,1,0:T(4,128)(2,1)S(1)} %bitcast.266), channel_id=1, replica_groups=mesh['dp_0'=4,'dp_1'=4,'vocab_0'=4,'vocab_1'=2] {'dp_0','dp_1','vocab_0'..., dimensions={0} | all-to-all | bytes 786432 | tf_op jit(solution)/shard_map/all_to_all | solution.py:131
  35.3 7.9 %convolution_convert_fusion = bf16[384,7168]{1,0:T(8,128)(2,1)} fusion(bf16[384,512]{1,0:T(8,128)(2,1)S(1)} %reshape.798, bf16[1,512,7168]{2,1,0:T(8,128)(2,1)} %param.14), kind=kOutput, calls=%fused_computation | convolution fusion | flops 2821324800 | bytes 13238272 | tf_op jit(solution)/shard_map/dot_general | solution.py:133
  43.2 12.3 %reshape.799 = bf16[128,3,7168]{2,1,0:T(4,128)(2,1)} reshape(bf16[384,7168]{1,0:T(8,128)(2,1)} %convolution_convert_fusion) | data formatting | bytes 11010048 | tf_op jit(solution)/shard_map/reshape | solution.py:139
  55.5 5.7 %all-to-all-start.1 = ((bf16[128,3,7168]{2,1,0:T(4,128)(2,1)}), bf16[128,3,7168]{2,1,0:T(4,128)(2,1)}, u32[]{:S(2)}, u32[]{:S(2)}) async-start(bf16[128,3,7168]{2,1,0:T(4,128)(2,1)} %reshape.799), calls=%async_computation.1 | async-start | bytes 14680064 | tf_op jit(solution)/shard_map/all_to_all | solution.py:138
  61.3 88.6 %all-to-all-done.1 = bf16[128,3,7168]{2,1,0:T(4,128)(2,1)} async-done(((bf16[128,3,7168]{2,1,0:T(4,128)(2,1)}), bf16[128,3,7168]{2,1,0:T(4,128)(2,1)}, u32[]{:S(2)}, u32[]{:S(2)}) %all-to-all-start.1) | async-done | bytes 5505056 | tf_op jit(solution)/shard_map/all_to_all | solution.py:138
  149.9 8.7 %slice_bitcast_fusion = (bf16[64,1,3,7168]{3,2,0,1:T(4,128)(2,1)}, bf16[64,1,3,7168]{3,2,0,1:T(4,128)(2,1)}) fusion(bf16[64,2,3,7168]{3,2,1,0:T(4,128)(2,1)} %bitcast.3), kind=kLoop, calls=%fused_computation.7 | loop fusion | bytes 11010048
  158.6 7.1 %reshape_squeeze.6 = bf16[192,7168]{1,0:T(8,128)(2,1)} reshape(bf16[64,1,3,7168]{3,2,0,1:T(4,128)(2,1)} %get-tuple-element.18) | data formatting | bytes 5505024 | tf_op jit(solution)/shard_map/reshape;squeeze | solution.py:143
  165.7 4.3 %fusion.9 = f32[128,7168]{1,0:T(8,128)} fusion(bf16[192,7168]{1,0:T(8,128)(2,1)} %reshape_squeeze.6, s32[128]{0:T(128)S(1)} %multiply_add_fusion), kind=kOutput, calls=%fused_computation.23 | convolution fusion | flops 352346112 | bytes 6423040 | tf_op jit(solution)/shard_map/dot_general | solution.py:146
  169.9 7.1 %reshape_squeeze.7 = bf16[192,7168]{1,0:T(8,128)(2,1)} reshape(bf16[64,1,3,7168]{3,2,0,1:T(4,128)(2,1)} %get-tuple-element.17) | data formatting | bytes 5505024 | tf_op jit(solution)/shard_map/reshape;squeeze | solution.py:144
  177.0 4.4 %fusion.3 = f32[16,7168]{1,0:T(8,128)S(1)} fusion(f32[16,8]{1,0:T(8,128)S(1)} %copy.26, f32[128,7168]{1,0:T(8,128)} %fusion.9, bf16[192,7168]{1,0:T(8,128)(2,1)} %reshape_squeeze.7, s32[128]{0:T(128)S(1)} %multiply_add_fusion), kind=kOutput, calls=%fused_computation.9 | convolution fusion | flops 354983936 | bytes 6882304 | tf_op jit(solution)/shard_map/dot_general | solution.py:147
  181.4 1.1 fusion.4
  182.6 0.8 fusion.6
  183.4 1.4 broadcast_in_dim.5
  184.8 6.1 %all-to-all-start.2 = ((bf16[8,16,7168]{2,1,0:T(8,128)(2,1)}), bf16[8,16,7168]{2,1,0:T(8,128)(2,1)S(1)}, u32[]{:S(2)}, u32[]{:S(2)}) async-start(bf16[8,16,7168]{2,1,0:T(8,128)(2,1)} %broadcast_in_dim.5), calls=%async_computation.2 | async-start | bytes 3670016 | tf_op jit(solution)/shard_map/all_to_all | solution.py:20
  191.2 83.7 %all-reduce = s32[2048]{0:T(1024)S(1)} all-reduce(s32[2048]{0:T(1024)S(1)} %dynamic-slice_dynamic-update-slice_fusion), channel_id=1, replica_groups=mesh['dp_0'=4,'dp_1'=4,'vocab_0'=4,'vocab_1'=2] {'dp_0','dp_1','vocab_0'..., use_global_device_ids=true, to_apply=%add | all-reduce | flops 2048 | bytes 16384
  274.9 16.3 %all-gather.10.cloned.1.call-done = bf16[2048,7168]{1,0:T(8,128)(2,1)} async-done(((bf16[16,7168]{1,0:T(8,128)(2,1)}), bf16[2048,7168]{1,0:T(8,128)(2,1)}) %all-gather.10.cloned.1.call-update) | async-done | bytes 29360144 | tf_op jit(solution)/shard_map/all_gather | solution.py:159
  291.2 34.9 %fusion.60 = (f32[2048]{0:T(1024)S(1)}, f32[2048,896]{0,1:T(8,128)}) fusion(bf16[2048,7168]{1,0:T(8,128)(2,1)} %all-gather.10.cloned.1.call-done, bf16[7168,896]{1,0:T(8,128)(2,1)} %param.16), kind=kOutput, calls=%fused_computation.124 | convolution fusion | flops 26308507648 | bytes 49553408 | tf_op jit(solution)/shard_map/dot_general | solution.py:161
  326.1 4.3 %exponential_reduce_fusion = (f32[2048]{0:T(1024)S(1)}, f32[2048]{0:T(1024)S(1)}) fusion(f32[2048,896]{0,1:T(8,128)} %get-tuple-element.25, f32[2048]{0:T(1024)S(1)} %get-tuple-element.24, s32[2048]{0:T(1024)S(1)} %all-reduce, s32[896]{0:T(1024)S(1)} %iota_add_fusion), kind=kLoop, calls=%fused_computation.6 | loop fusion | flops 9170944 | bytes 7376384 | tf_op jit(solution)/shard_map/reduce_sum | solution.py:163
  330.4 9.9 %all-gather.4 = f32[4,3,2048]{2,1,0:T(4,128)S(1)} all-gather(f32[1,3,2048]{2,1,0:T(4,128)S(1)} %maximum_bitcast_fusion), channel_id=2, replica_groups=mesh['dp_0'=4,'dp_1'=4,'vocab_0'=4,'vocab_1'=2] {'dp_0'}, dimensions={0}, use_global_device_ids=true | all-gather | bytes 122880 | tf_op jit(solution)/shard_map/all_gather | solution.py:44
  340.4 9.1 %all-gather.5 = f32[4,3,2048]{2,1,0:T(4,128)S(1)} all-gather(f32[1,3,2048]{2,1,0:T(4,128)S(1)} %maximum_bitcast_fusion.1), channel_id=3, replica_groups=mesh['dp_0'=4,'dp_1'=4,'vocab_0'=4,'vocab_1'=2] {'dp_1'}, dimensions={0}, use_global_device_ids=true | all-gather | bytes 122880 | tf_op jit(solution)/shard_map/all_gather | solution.py:44
  349.7 9.7 %all-gather.6 = f32[4,3,2048]{2,1,0:T(4,128)S(1)} all-gather(f32[1,3,2048]{2,1,0:T(4,128)S(1)} %maximum_bitcast_fusion.2), channel_id=4, replica_groups=mesh['dp_0'=4,'dp_1'=4,'vocab_0'=4,'vocab_1'=2] {'vocab_0'}, dimensions={0}, use_global_device_ids=true | all-gather | bytes 122880 | tf_op jit(solution)/shard_map/all_gather | solution.py:44
  359.5 9.7 %all-gather.7 = f32[2,3,2048]{2,1,0:T(4,128)S(1)} all-gather(f32[1,3,2048]{2,1,0:T(4,128)S(1)} %maximum_bitcast_fusion.3), channel_id=5, replica_groups=mesh['dp_0'=4,'dp_1'=4,'vocab_0'=4,'vocab_1'=2] {'vocab_1'}, dimensions={0}, use_global_device_ids=true | all-gather | bytes 73728 | tf_op jit(solution)/shard_map/all_gather | solution.py:44
  370.0 1.2 copy.33
  (55 shorter events, 3.8 us)
Async XLA Ops:
  7.2 1.6 copy-start
  55.5 5.7 %copy-start.5 = (f32[128,8]{0,1:T(8,128)S(1)}, f32[128,8]{0,1:T(8,128)}, u32[]{:S(2)}) copy-start(f32[128,8]{0,1:T(8,128)} %param.13) | copy-start | bytes 12292
  55.5 94.5 %all-to-all-start.1 = ((bf16[128,3,7168]{2,1,0:T(4,128)(2,1)}), bf16[128,3,7168]{2,1,0:T(4,128)(2,1)}, u32[]{:S(2)}, u32[]{:S(2)}) async-start(bf16[128,3,7168]{2,1,0:T(4,128)(2,1)} %reshape.799), calls=%async_computation.1 | async-start | bytes 14680064 | tf_op jit(solution)/shard_map/all_to_all | solution.py:138
  61.1 230.0 %all-gather.10.cloned.1.call-start = ((), (), s32[]{:S(2)}) async-start(), calls=%async_computation.3 | async-start | bytes 29589504 | tf_op jit(solution)/shard_map/all_gather | solution.py:159
  177.0 5.6 %copy-start.4 = (f32[7168]{0:T(1024)S(1)}, f32[7168]{0:T(1024)}, u32[]{:S(2)}) copy-start(f32[7168]{0:T(1024)} %param.15) | copy-start | bytes 86020
  177.0 14.0 %copy-start.6 = (s32[128]{0:T(128)S(1)}, s32[128]{0:T(128)}, u32[]{:S(2)}) copy-start(s32[128]{0:T(128)} %param.17) | copy-start | bytes 1540
  184.8 90.0 %all-to-all-start.2 = ((bf16[8,16,7168]{2,1,0:T(8,128)(2,1)}), bf16[8,16,7168]{2,1,0:T(8,128)(2,1)S(1)}, u32[]{:S(2)}, u32[]{:S(2)}) async-start(bf16[8,16,7168]{2,1,0:T(8,128)(2,1)} %broadcast_in_dim.5), calls=%async_computation.2 | async-start | bytes 3670016 | tf_op jit(solution)/shard_map/all_to_all | solution.py:20
  274.9 51.2 %copy-start.2 = (bf16[8,16,7168]{2,1,0:T(8,128)(2,1)}, bf16[8,16,7168]{2,1,0:T(8,128)(2,1)S(1)}, u32[]{:S(2)}) copy-start(bf16[8,16,7168]{2,1,0:T(8,128)(2,1)S(1)} %all-to-all-done.2) | copy-start | bytes 5505028
  326.0 43.3 %copy-start.7 = (f32[128]{0:T(128)S(1)}, f32[128]{0:T(128)}, u32[]{:S(2)}) copy-start(f32[128]{0:T(128)} %param.19) | copy-start | bytes 1540
  326.0 43.3 %copy-start.8 = (f32[128]{0:T(128)S(1)}, f32[128]{0:T(128)}, u32[]{:S(2)}) copy-start(f32[128]{0:T(128)} %param.18) | copy-start | bytes 1540
  326.0 43.9 %copy-start.3 = (bf16[8,16,7168]{2,1,0:T(8,128)(2,1)S(1)}, bf16[8,16,7168]{2,1,0:T(8,128)(2,1)}, u32[]{:S(2)}) copy-start(bf16[8,16,7168]{2,1,0:T(8,128)(2,1)} %copy-done.2) | copy-start | bytes 5505028
  326.0 45.1 %copy-start.1 = (bf16[128,8,1024]{2,1,0:T(8,128)(2,1)S(1)}, bf16[128,8,1024]{2,1,0:T(8,128)(2,1)}, u32[]{:S(2)}) copy-start(bf16[128,8,1024]{2,1,0:T(8,128)(2,1)} %param.11) | copy-start | bytes 6291460
Sparse Core Ops, SparseCore 0:
  183.5 107.5 all-gather.9
where the time goes:
time: 379 us; the launch traced here: 378 us
  blocking collectives  147 us (39%)
  waiting for transfers between devices  105 us (28%)
  matrix products  51.9 us (14%)
  local copies, waits for them, and re-layouts  40 us (11%)
  between operations  14.3 us (4%)
  starting transfers between devices  11.8 us (3%)
  other arithmetic  8.19 us (2%)
    all_to_all x1, waiting for transfers between devices, per_device(): lax.all_to_all(product.reshape(sources, slot_count, -1), DP_VOCAB, split_...  88.6 us
    unnamed x1, blocking collectives  83.7 us
    all_gather x4, blocking collectives, all_in_one(): both, at, found = (lax.all_gather(jnp.concatenate(lines), axis), 0, {})  38.3 us
    dot_general x1, matrix products, per_device(): logits = jnp.dot(normed, head_weight, preferred_element_type=jnp.float32)  34.9 us
    all_to_all x1, blocking collectives, per_device(): lax.all_to_all(buffer, DP_VOCAB, split_axis=0, concat_axis=0, tiled=True)  24.9 us
    all_gather x1, waiting for transfers between devices, per_device(): normed = lax.all_gather(normed_sub, DP_VOCAB, axis=0, tiled=True)  16.3 us
    reshape x1, local copies, waits for them, and re-layouts, per_device(): product.reshape(sources, slot_count, -1)  12.3 us
    unnamed x22, local copies, waits for them, and re-layouts  10.2 us
  transfers between devices with their start and end apart: 3, of which 2 were waited for; matrix products, arithmetic and copies ran while one was open for 0% of the time, Pallas kernels for 0%

commit v1 on v0

v1 whole, which is shorter than its diff:
```python
import jax
import jax.numpy as jnp
from jax import lax
from jax.sharding import Mesh
from jax.sharding import PartitionSpec as P

X = "vocab_0"
CORE = "vocab_1"
VOCAB = ("vocab_0", "vocab_1")
DP_VOCAB = ("dp_0", "dp_1", "vocab_0", "vocab_1")
DP = ("dp_0", "dp_1")

norm_epsilon = 1e-06
clip_low = 0.8
clip_high = 1.2
dual_bound = 3.0
bf16 = jnp.bfloat16
f32 = jnp.float32


def clipped_loss(logprob, rollout_logprob, advantages):
    ratio = jnp.exp(logprob - rollout_logprob)
    surrogate = jnp.minimum(ratio * advantages, jnp.clip(ratio, clip_low, clip_high) * advantages)
    bounded = jnp.where(
        advantages < 0.0, jnp.maximum(surrogate, dual_bound * advantages), surrogate
    )
    return -bounded


def dot(a, b):
    return jnp.dot(a, b, preferred_element_type=f32)


def swap_cores(x):
    return lax.ppermute(x, CORE, [(0, 1), (1, 0)])


def label_row(targets):
    digits = [(targets // 128**k) % 128 for k in range(3)]
    row = jnp.concatenate(digits + [jnp.zeros_like(targets)]).astype(bf16)
    return row[None]


def labels_of(rows):
    digits = rows.astype(f32).astype(jnp.int32).reshape(rows.shape[0], 4, 128)
    return digits[:, 0] + 128 * digits[:, 1] + 128 * 128 * digits[:, 2]


def experts_stage(tokens, expert_hidden, routes, route_weight, expert_weight, targets):
    x, h = lax.axis_index(X), lax.axis_index(CORE)
    rows, top = routes.shape
    width = expert_hidden.shape[2] // 2
    cols = tokens.shape[1] // 2
    blocks = rows // 16
    by_block = routes.reshape(blocks, 16 * top).T
    mine = (
        by_block[:, :, None] == (lax.iota(jnp.int32, 16) * 4 + x)[None, None, :]
    ).astype(bf16)
    n = 16 * top
    lower = (lax.iota(jnp.int32, n)[:, None] > lax.iota(jnp.int32, n)[None, :]).astype(bf16)
    before = dot(lower, mine.reshape(n, blocks * 16)).reshape(n, blocks, 16)
    slot = jnp.sum(before * mine.astype(f32), axis=2).astype(jnp.int32)
    place = (by_block // 4) * 24 + lax.iota(jnp.int32, blocks)[None, :] * 3 + slot
    place = jnp.where(by_block % 4 == x, place, -1).T.reshape(rows, top)
    select = (lax.iota(jnp.int32, 384)[:, None] == place.reshape(-1)[None, :]).astype(bf16)
    hidden = lax.dynamic_slice_in_dim(
        expert_hidden.reshape(rows * top, 2 * width), h * width, width, 1
    )
    buffer = dot(select, hidden).astype(bf16).reshape(16, 24, width)
    extra = jnp.pad(label_row(targets), ((0, 7), (0, 0)))
    buffer = jnp.concatenate(
        [buffer, jnp.broadcast_to(extra[None], (16, 8, width))], axis=1
    )
    received = lax.all_to_all(buffer, DP, 0, 0, tiled=True)
    labels = labels_of(received[:, 24])
    own = received[:, :24].reshape(384, width)
    other = swap_cores(own)
    weight = expert_weight[0]
    weight_own = lax.dynamic_slice_in_dim(weight, h * cols, cols, 1)
    weight_other = swap_cores(lax.dynamic_slice_in_dim(weight, (1 - h) * cols, cols, 1))
    product = (dot(own, weight_own) + dot(other, weight_other)).astype(bf16)
    back = lax.all_to_all(product.reshape(16, 24, cols), DP, 0, 0, tiled=True)
    gate = jnp.sum(
        jnp.where(
            place[:, :, None] == lax.iota(jnp.int32, 384)[None, None, :],
            route_weight[:, :, None],
            0.0,
        ),
        axis=1,
    )
    gate_high = gate.astype(bf16)
    gate_low = (gate - gate_high.astype(f32)).astype(bf16)
    both = dot(jnp.concatenate([gate_high, gate_low]), back.reshape(384, cols))
    partial = (both[:rows] + both[rows:]).astype(bf16)
    parts = lax.all_to_all(partial.reshape(4, rows // 4, cols), X, 0, 0, tiled=True)
    moe = jnp.sum(parts.astype(f32), axis=0)
    mine_tokens = lax.dynamic_slice(tokens, (x * (rows // 4), h * cols), (rows // 4, cols))
    return (mine_tokens.astype(f32) + moe).astype(bf16), labels


def combined(peaks, totals, picks):
    peak = jnp.max(peaks, axis=0)
    return peak, jnp.sum(totals * jnp.exp(peaks - peak), axis=0), jnp.sum(picks, axis=0)


def per_device(
    tokens,
    expert_hidden,
    routes,
    route_weight,
    expert_weight,
    norm_gain,
    head_weight,
    targets,
    rollout_logprob,
    advantages,
):
    h = lax.axis_index(CORE)
    tile, labels = experts_stage(
        tokens, expert_hidden, routes, route_weight, expert_weight, targets
    )
    sub, cols = tile.shape[0] // 2, tile.shape[1]
    kept = lax.dynamic_slice_in_dim(tile, h * sub, sub, 0)
    got = swap_cores(lax.dynamic_slice_in_dim(tile, (1 - h) * sub, sub, 0))
    layer_sub = jnp.where(
        h == 0, jnp.concatenate([kept, got], axis=1), jnp.concatenate([got, kept], axis=1)
    )
    group_layer = lax.all_to_all(
        jnp.broadcast_to(layer_sub[None], (8, *layer_sub.shape)), VOCAB, 0, 0, tiled=True
    ).reshape(tokens.shape)
    widened = layer_sub.astype(f32)
    mean_square = jnp.mean(widened * widened, axis=-1, keepdims=True)
    normed_sub = (widened * lax.rsqrt(mean_square + norm_epsilon) * norm_gain).astype(bf16)
    voc_dev = head_weight.shape[1]
    columns = lax.axis_index(DP_VOCAB) * voc_dev + lax.iota(jnp.int32, voc_dev)
    by_device = labels.reshape(-1, 2, sub // 2)
    stats = []
    for c in range(2):
        piece = normed_sub[c * (sub // 2) : (c + 1) * (sub // 2)]
        normed = lax.all_gather(piece, DP_VOCAB, axis=0, tiled=True)
        logits = dot(normed, head_weight)
        peak = jnp.max(logits, axis=1)
        total = jnp.sum(jnp.exp(logits - peak[:, None]), axis=1)
        wanted = by_device[:, c].reshape(-1)
        picked = jnp.sum(jnp.where(columns[None, :] == wanted[:, None], logits, 0.0), axis=1)
        stats.append(jnp.stack([peak, total, picked]).reshape(3, -1, 1, sub // 2))
    stats = jnp.concatenate(stats, axis=2).reshape(3, 16, -1).transpose(1, 0, 2)
    sent = lax.all_to_all(stats, DP, 0, 0, tiled=True)
    group = jnp.stack(combined(sent[:, 0], sent[:, 1], sent[:, 2]))
    sent = lax.all_gather(group, VOCAB, axis=0)
    peak, total, target_logit = combined(sent[:, 0], sent[:, 1], sent[:, 2])
    token_logprob = target_logit - (peak + jnp.log(total))
    token_loss = clipped_loss(token_logprob, rollout_logprob, advantages)
    return (group_layer, token_logprob, token_loss)


def solution(mesh):
    torus = Mesh(mesh.devices.reshape(4, 4, 4, 2), ("dp_0", "dp_1", "vocab_0", "vocab_1"))
    placed = (
        P(DP, None),
        P(DP, None, None),
        P(DP, None),
        P(DP, None),
        P(DP_VOCAB, None, None),
        P(),
        P(None, DP_VOCAB),
        P(DP),
        P(DP),
        P(DP),
    )
    return jax.shard_map(
        per_device,
        mesh=torus,
        in_specs=placed,
        out_specs=(P(DP, None), P(DP), P(DP)),
        check_vma=False,
    )
```

time: 379 us -> 331 us (0.87)
  blocking collectives: 147 us -> 30.6 us
  waiting for transfers between devices: 105 us -> 187 us
  local copies, waits for them, and re-layouts: 40 us -> 12.8 us
  starting transfers between devices: 11.8 us -> 24.8 us
    all_gather x1 -> x2, waiting for transfers between devices: 16.3 us -> 130 us  [per_device(): normed = lax.all_gather(piece, DP_VOCAB, axis=0, tiled=True)]
    unnamed x1 -> x0, blocking collectives: 83.7 us -> none
    all_to_all x2 -> x4, waiting for transfers between devices: 88.6 us -> 55.2 us  [the longest x1 36.7 us: experts_stage(): back = lax.all_to_all(product.reshape(16, 24, cols), DP, 0, 0, tiled=True)]
    all_gather x4 -> x1, blocking collectives: 38.3 us -> 12.8 us  [per_device(): sent = lax.all_gather(group, VOCAB, axis=0)]
    another operation x4 -> x12, local copies, waits for them, and re-layouts: 14.4 us -> 0.88 us  [per_device(): stats.append(jnp.stack([peak, total, picked]).reshape(3, -1, 1, sub // 2))]
    reshape x5 -> x2, local copies, waits for them, and re-layouts: 12.9 us -> 0.62 us  [the longest x1 0.53 us: per_device(): stats = jnp.concatenate(stats, axis=2).reshape(3, 16, -1).transpose(1, 0, 2)]
    unnamed x22 -> x19, local copies, waits for them, and re-layouts: 10.2 us -> 3.09 us
    all_to_all x1, blocking collectives: 24.9 us -> 17.8 us  [experts_stage(): received = lax.all_to_all(buffer, DP, 0, 0, tiled=True)]
  transfers between devices with their start and end apart: 3 -> 9, of which waited for: 2 -> 6; matrix products, arithmetic and copies ran while one was open for 0% -> 17% of each run, Pallas kernels for 0% -> 0%
where the time goes in v1:
time: 331 us; the launch traced here: 330 us
  waiting for transfers between devices  187 us (56%)
  matrix products  52.2 us (16%)
  blocking collectives  30.6 us (9%)
  starting transfers between devices  24.8 us (7%)
  between operations  14.4 us (4%)
  local copies, waits for them, and re-layouts  12.8 us (4%)
  other arithmetic  8.41 us (3%)
    all_gather x2, waiting for transfers between devices, per_device(): normed = lax.all_gather(piece, DP_VOCAB, axis=0, tiled=True)  130 us
    dot_general x7, matrix products, dot(): return jnp.dot(a, b, preferred_element_type=f32)  52.2 us
    all_to_all x1, waiting for transfers between devices, experts_stage(): back = lax.all_to_all(product.reshape(16, 24, cols), DP, 0, 0, tiled=True)  36.7 us
    all_to_all x1, blocking collectives, experts_stage(): received = lax.all_to_all(buffer, DP, 0, 0, tiled=True)  17.8 us
    all_gather x1, blocking collectives, per_device(): sent = lax.all_gather(group, VOCAB, axis=0)  12.8 us
    all_to_all x1, waiting for transfers between devices, experts_stage(): lax.all_to_all(partial.reshape(4, rows // 4, cols), X, 0, 0, tiled=True)  12 us
  transfers between devices with their start and end apart: 9, of which 6 were waited for; matrix products, arithmetic and copies ran while one was open for 17% of the time, Pallas kernels for 0%

profile of v1, /device:TPU:1, one launch (start us, length us, event | category | flops | bytes accessed | tf_op | source)
XLA Modules:
  0.0 330.1 jit_solution(12316371568212583948)
XLA Ops:
  7.2 4.3 %dynamic-slice_bitcast_fusion = bf16[512,3584]{1,0:T(8,128)(2,1)} fusion(bf16[1,512,7168]{2,1,0:T(8,128)(2,1)} %param.14, s32[]{:T(128)S(6)} %select_n.101), kind=kLoop, calls=%fused_computation.8 | loop fusion | bytes 7340036 | tf_op jit(solution)/shard_map/dynamic_slice | solution.py:80
  11.5 1.4 collective-permute-start.1
  14.2 17.8 %all_to_all.25 = bf16[16,32,512]{2,1,0:T(8,128)(2,1)S(1)} all-to-all(bf16[16,32,512]{2,1,0:T(8,128)(2,1)S(1)} %pad_maximum_fusion), channel_id=1, replica_groups=mesh['dp_0'=4,'dp_1'=4,'vocab_0'=4,'vocab_1'=2] {'dp_0','dp_1'}, dimensions={0} | all-to-all | bytes 1048576 | tf_op jit(solution)/shard_map/all_to_all | solution.py:74
  32.1 2.4 collective-permute-start
  34.5 3.6 %fusion.1 = f32[384,3584]{1,0:T(8,128)S(1)} fusion(bf16[384,512]{1,0:T(8,128)(2,1)S(1)} %bitcast.58, bf16[1,512,7168]{2,1,0:T(8,128)(2,1)} %param.14, s32[]{:T(128)S(6)} %select_n.90), kind=kOutput, calls=%fused_computation.2 | convolution fusion | flops 1409286144 | bytes 9568260 | tf_op jit(solution)/shard_map/dot_general | solution.py:31
  38.1 5.2 %fusion = bf16[384,3584]{1,0:T(8,128)(2,1)} fusion(f32[384,3584]{1,0:T(8,128)S(1)} %fusion.1, bf16[384,512]{1,0:T(8,128)(2,1)S(1)} %collective-permute-done, bf16[512,3584]{1,0:T(8,128)(2,1)} %collective-permute-done.1), kind=kOutput, calls=%fused_computation.1 | convolution fusion | flops 1412038656 | bytes 12320768 | tf_op jit(solution)/shard_map/dot_general | solution.py:31
  43.3 3.9 %all-to-all-start.1 = ((bf16[16,24,3584]{2,1,0:T(8,128)(2,1)}), bf16[16,24,3584]{2,1,0:T(8,128)(2,1)S(1)}, u32[]{:S(2)}, u32[]{:S(2)}) async-start(bf16[16,24,3584]{2,1,0:T(8,128)(2,1)} %bitcast.56), calls=%async_computation.1 | async-start | bytes 5505024 | tf_op jit(solution)/shard_map/all_to_all | solution.py:82
  48.0 36.7 %all-to-all-done.1 = bf16[16,24,3584]{2,1,0:T(8,128)(2,1)S(1)} async-done(((bf16[16,24,3584]{2,1,0:T(8,128)(2,1)}), bf16[16,24,3584]{2,1,0:T(8,128)(2,1)S(1)}, u32[]{:S(2)}, u32[]{:S(2)}) %all-to-all-start.1) | async-done | bytes 2752544 | tf_op jit(solution)/shard_map/all_to_all | solution.py:82
  84.7 1.1 fusion.13
  85.8 1.1 fusion.4
  86.9 4.1 %all-to-all-start.2 = ((bf16[4,32,3584]{2,1,0:T(8,128)(2,1)}), bf16[4,32,3584]{2,1,0:T(8,128)(2,1)S(1)}, u32[]{:S(2)}, u32[]{:S(2)}) async-start(bf16[4,32,3584]{2,1,0:T(8,128)(2,1)} %bitcast.17), calls=%async_computation.2 | async-start | bytes 1835008 | tf_op jit(solution)/shard_map/all_to_all | solution.py:95
  91.0 12.0 %all-to-all-done.2 = bf16[4,32,3584]{2,1,0:T(8,128)(2,1)S(1)} async-done(((bf16[4,32,3584]{2,1,0:T(8,128)(2,1)}), bf16[4,32,3584]{2,1,0:T(8,128)(2,1)S(1)}, u32[]{:S(2)}, u32[]{:S(2)}) %all-to-all-start.2) | async-done | bytes 917536 | tf_op jit(solution)/shard_map/all_to_all | solution.py:95
  104.2 2.7 collective-permute-start.2
  110.6 1.4 broadcast_in_dim.25
  112.0 4.6 %all-to-all-start.3 = ((bf16[8,16,7168]{2,1,0:T(8,128)(2,1)}), bf16[8,16,7168]{2,1,0:T(8,128)(2,1)}, u32[]{:S(2)}, u32[]{:S(2)}) async-start(bf16[8,16,7168]{2,1,0:T(8,128)(2,1)} %broadcast_in_dim.25), calls=%async_computation.3 | async-start | bytes 3670016 | tf_op jit(solution)/shard_map/all_to_all | solution.py:128
  116.6 71.4 %all-gather.5.cloned.1.call-done = bf16[1024,7168]{1,0:T(8,128)(2,1)} async-done(((bf16[8,7168]{1,0:T(8,128)(2,1)}), bf16[1024,7168]{1,0:T(8,128)(2,1)}) %all-gather.5.cloned.1.call-update) | async-done | bytes 14680080 | tf_op jit(solution)/shard_map/all_gather | solution.py:140
  188.0 20.6 %fusion.44 = (f32[1024]{0:T(1024)S(1)}, f32[1024,896]{0,1:T(8,128)}) fusion(bf16[1024,7168]{1,0:T(8,128)(2,1)} %all-gather.5.cloned.1.call-done, bf16[7168,896]{1,0:T(8,128)(2,1)} %param.16), kind=kOutput, calls=%fused_computation.106 | convolution fusion | flops 13154253824 | bytes 31199232 | tf_op jit(solution)/shard_map/dot_general | solution.py:31
  208.7 58.5 %all-gather.7.cloned.1.call-done = bf16[1024,7168]{1,0:T(8,128)(2,1)} async-done(((bf16[8,7168]{1,0:T(8,128)(2,1)}), bf16[1024,7168]{1,0:T(8,128)(2,1)}) %all-gather.7.cloned.1.call-update) | async-done | bytes 14680080 | tf_op jit(solution)/shard_map/all_gather | solution.py:140
  267.2 20.9 %fusion.45 = (f32[1024]{0:T(1024)S(1)}, f32[1024,896]{0,1:T(8,128)}) fusion(bf16[1024,7168]{1,0:T(8,128)(2,1)} %all-gather.7.cloned.1.call-done, bf16[7168,896]{1,0:T(8,128)(2,1)} %param.16), kind=kOutput, calls=%fused_computation.107 | convolution fusion | flops 13154253824 | bytes 31199232 | tf_op jit(solution)/shard_map/dot_general | solution.py:31
  288.3 4.3 %exponential_reduce_fusion.1 = (f32[1024]{0:T(1024)S(1)}, f32[1024]{0:T(1024)S(1)}, f32[1024]{0:T(1024)S(1)}, f32[1024]{0:T(1024)S(1)}) fusion(f32[1024,896]{0,1:T(8,128)} %get-tuple-element.32, f32[1024]{0:T(1024)S(1)} %get-tuple-element.31, s32[1024]{0:T(1024)S(1)} %eq.118, s32[896]{0:T(1024)S(1)} %iota_add_fusion, f32[1024,896]{0,1:T(8,128)} %get-tuple-element.34, ...), kind=kLoop, calls=%fused_computation.7 | loop fusion | flops 9170944 | bytes 7376384 | tf_op jit(solution)/shard_map/reduce_sum | solution.py:143
  294.7 5.7 %all-to-all-start.4 = ((f32[16,3,128]{2,1,0:T(4,128)}), f32[16,3,128]{2,1,0:T(4,128)S(1)}, u32[]{:S(2)}, u32[]{:S(2)}) async-start(f32[16,3,128]{2,1,0:T(4,128)} %copy.49), calls=%async_computation.4 | async-start | bytes 65536 | tf_op jit(solution)/shard_map/all_to_all | solution.py:148
  300.5 6.5 %all-to-all-done.4 = f32[16,3,128]{2,1,0:T(4,128)S(1)} async-done(((f32[16,3,128]{2,1,0:T(4,128)}), f32[16,3,128]{2,1,0:T(4,128)S(1)}, u32[]{:S(2)}, u32[]{:S(2)}) %all-to-all-start.4) | async-done | bytes 24608 | tf_op jit(solution)/shard_map/all_to_all | solution.py:148
  307.0 12.8 %all-gather.1 = f32[8,3,128]{2,1,0:T(4,128)S(1)} all-gather(f32[1,3,128]{2,1,0:T(4,128)S(1)} %maximum_bitcast_fusion), channel_id=2, replica_groups=mesh['dp_0'=4,'dp_1'=4,'vocab_0'=4,'vocab_1'=2] {'vocab_0','vocab_1'}, dimensions={0}, use_global_device_ids=true | all-gather | bytes 13824 | tf_op jit(solution)/shard_map/all_gather | solution.py:150
  320.5 2.8 copy.55
  (83 shorter events, 9.8 us)
Async XLA Ops:
  7.2 6.4 %copy-start = (bf16[128,8,1024]{2,1,0:T(8,128)(2,1)S(1)}, bf16[128,8,1024]{2,1,0:T(8,128)(2,1)}, u32[]{:S(2)}) copy-start(bf16[128,8,1024]{2,1,0:T(8,128)(2,1)} %param.11) | copy-start | bytes 6291460
  7.2 5.8 %copy-start.7 = (s32[128]{0:T(128)S(1)}, s32[128]{0:T(128)}, u32[]{:S(2)}) copy-start(s32[128]{0:T(128)} %param.17) | copy-start | bytes 1540
  7.2 5.8 %copy-start.3 = (s32[128,8]{0,1:T(8,128)S(1)}, s32[128,8]{0,1:T(8,128)}, u32[]{:S(2)}) copy-start(s32[128,8]{0,1:T(8,128)} %param.12) | copy-start | bytes 12292
  11.5 26.7 %collective-permute-start.1 = (bf16[512,3584]{1,0:T(8,128)(2,1)}, bf16[512,3584]{1,0:T(8,128)(2,1)}, u32[]{:S(2)}, u32[]{:S(2)}) collective-permute-start(bf16[512,3584]{1,0:T(8,128)(2,1)} %dynamic-slice_bitcast_fusion), channel_id=1, source_target_pairs={{0,1},{1,0},{2,3},{3,2},{4,5},{5,4},{6,7},{7,6},{8,9},{9,8},{10,11... | collective-permute-start | bytes 11010056 | tf_op jit(solution)/shard_map/ppermute | solution.py:35
  32.1 6.0 %collective-permute-start = (bf16[384,512]{1,0:T(8,128)(2,1)S(1)}, bf16[384,512]{1,0:T(8,128)(2,1)S(1)}, u32[]{:S(2)}, u32[]{:S(2)}) collective-permute-start(bf16[384,512]{1,0:T(8,128)(2,1)S(1)} %bitcast.57), channel_id=1, source_target_pairs={{0,1},{1,0},{2,3},{3,2},{4,5},{5,4},{6,7},{7,6},{8,9},{9,8},{10,11... | collective-permute-start | bytes 1179656 | tf_op jit(solution)/shard_map/ppermute | solution.py:35
  43.3 4.0 %copy-start.4 = (f32[128,8]{0,1:T(8,128)S(1)}, f32[128,8]{0,1:T(8,128)}, u32[]{:S(2)}) copy-start(f32[128,8]{0,1:T(8,128)} %param.13) | copy-start | bytes 12292
  43.3 41.4 %all-to-all-start.1 = ((bf16[16,24,3584]{2,1,0:T(8,128)(2,1)}), bf16[16,24,3584]{2,1,0:T(8,128)(2,1)S(1)}, u32[]{:S(2)}, u32[]{:S(2)}) async-start(bf16[16,24,3584]{2,1,0:T(8,128)(2,1)} %bitcast.56), calls=%async_computation.1 | async-start | bytes 5505024 | tf_op jit(solution)/shard_map/all_to_all | solution.py:82
  86.9 21.2 %copy-start.2 = (f32[7168]{0:T(1024)S(1)}, f32[7168]{0:T(1024)}, u32[]{:S(2)}) copy-start(f32[7168]{0:T(1024)} %param.15) | copy-start | bytes 86020
  86.9 16.2 %all-to-all-start.2 = ((bf16[4,32,3584]{2,1,0:T(8,128)(2,1)}), bf16[4,32,3584]{2,1,0:T(8,128)(2,1)S(1)}, u32[]{:S(2)}, u32[]{:S(2)}) async-start(bf16[4,32,3584]{2,1,0:T(8,128)(2,1)} %bitcast.17), calls=%async_computation.2 | async-start | bytes 1835008 | tf_op jit(solution)/shard_map/all_to_all | solution.py:95
  91.0 97.0 %all-gather.5.cloned.1.call-start = ((), (), s32[]{:S(2)}) async-start(), calls=%async_computation.5 | async-start | bytes 14794752 | tf_op jit(solution)/shard_map/all_gather | solution.py:140
  104.2 3.7 %collective-permute-start.2 = (bf16[16,3584]{1,0:T(8,128)(2,1)S(1)}, bf16[16,3584]{1,0:T(8,128)(2,1)S(1)}, u32[]{:S(2)}, u32[]{:S(2)}) collective-permute-start(bf16[16,3584]{1,0:T(8,128)(2,1)S(1)} %get-tuple-element.19), channel_id=1, source_target_pairs={{0,1},{1,0},{2,3},{3,2},{4,5},{5,4},{6,7},{7,6},{8,9},{9,8},{10,11... | collective-permute-start | bytes 344072 | tf_op jit(solution)/shard_map/ppermute | solution.py:35
  109.0 158.2 %all-gather.7.cloned.1.call-start = ((), (), s32[]{:S(2)}) async-start(), calls=%async_computation.6 | async-start | bytes 14794752 | tf_op jit(solution)/shard_map/all_gather | solution.py:140
  112.0 182.7 %all-to-all-start.3 = ((bf16[8,16,7168]{2,1,0:T(8,128)(2,1)}), bf16[8,16,7168]{2,1,0:T(8,128)(2,1)}, u32[]{:S(2)}, u32[]{:S(2)}) async-start(bf16[8,16,7168]{2,1,0:T(8,128)(2,1)} %broadcast_in_dim.25), calls=%async_computation.3 | async-start | bytes 3670016 | tf_op jit(solution)/shard_map/all_to_all | solution.py:128
  288.3 31.6 %copy-start.5 = (f32[128]{0:T(128)S(1)}, f32[128]{0:T(128)}, u32[]{:S(2)}) copy-start(f32[128]{0:T(128)} %param.19) | copy-start | bytes 1540
  288.3 31.6 %copy-start.6 = (f32[128]{0:T(128)S(1)}, f32[128]{0:T(128)}, u32[]{:S(2)}) copy-start(f32[128]{0:T(128)} %param.18) | copy-start | bytes 1540
  288.3 35.0 %copy-start.1 = (bf16[128,8,1024]{2,1,0:T(8,128)(2,1)S(1)}, bf16[128,8,1024]{2,1,0:T(8,128)(2,1)}, u32[]{:S(2)}) copy-start(bf16[128,8,1024]{2,1,0:T(8,128)(2,1)} %param.11) | copy-start | bytes 6291460
  294.7 12.2 %all-to-all-start.4 = ((f32[16,3,128]{2,1,0:T(4,128)}), f32[16,3,128]{2,1,0:T(4,128)S(1)}, u32[]{:S(2)}, u32[]{:S(2)}) async-start(f32[16,3,128]{2,1,0:T(4,128)} %copy.49), calls=%async_computation.4 | async-start | bytes 65536 | tf_op jit(solution)/shard_map/all_to_all | solution.py:148
Sparse Core Ops, SparseCore 0:
  109.1 78.8 all-gather.4
  191.0 76.1 all-gather.6
